TPU v7x, 256 devices: a whole 4x4x8 slice. The times are simulated.
256 devices in a mesh: seq: 32 (over x, z_lo, core), head: 8 (over y, z_hi).
Axes of the slice: x: 4, y: 4, z: 8 (z_hi: 2, z_lo: 4; z = z_hi * 4 + z_lo), core: 2. Of those that a mesh axis runs over, the one named last changes fastest.
Arguments:
- tokens: bfloat16 [16384, 1024], P('seq'), may hold values from -6 to 6
- mem_query_w: bfloat16 [1024, 1024], P(None, 'head'), may hold values from -0.1875 to 0.1875
- mem_key_w: bfloat16 [1024, 1024], P(None, 'head'), may hold values from -0.1875 to 0.1875
- mem_value_w: bfloat16 [1024, 1024], P(None, 'head'), may hold values from -0.1875 to 0.1875
- mem_in: float32 [1024, 1024], P(None, 'head'), may hold values from -0.1875 to 0.1875
- mem_out: float32 [1024, 1024], P('head'), may hold values from -0.1875 to 0.1875
- forget_levels: float32 [16, 1024], P(None, 'head'), may hold values from 0.003 to 0.3
- momentum_levels: float32 [16, 1024], P(None, 'head'), may hold values from 0.2 to 0.9
- step_levels: float32 [16, 1024], P(None, 'head'), may hold values from 0.02 to 0.2
- plan: int32 [32], P('seq'), may hold values from 0 to 15
- norm_gain: float32 [1024], replicated, may hold values from 0.5 to 1.5
- attn_query_w: bfloat16 [1024, 1024], P(None, 'head'), may hold values from -1 to 1
- attn_key_w: bfloat16 [1024, 1024], P(None, 'head'), may hold values from -4 to 4
- attn_value_w: bfloat16 [1024, 1024], P(None, 'head'), may hold values from -0.1875 to 0.1875
- attn_out_w: bfloat16 [1024, 1024], P('head'), may hold values from -0.25 to 0.25
Outputs:
- layer_out: bfloat16 [16384, 1024], P('seq', 'head')
All inputs are finite; a program needn't handle non-finite values.
Results may differ from a plain program's by a relative error of at most 0.014.
Values may be sent and summed in bfloat16 or wider, within the bound.
A program may use at most 128 MiB of HBM per device.

v0:
```python
import jax
import jax.numpy as jnp
from jax import lax
from jax.sharding import Mesh
from jax.sharding import PartitionSpec as P

HEAD_DIM = 64
SPAN = 8
SEQ = ("seq_0", "seq_1", "seq_2")
epsilon = 1e-06


def split_up(value, dim, length):
    before, after = (value.shape[:dim], value.shape[dim + 1 :])
    return jnp.moveaxis(value.reshape(*before, length, -1, *after), dim, 0)


def sent_and_summed(value, axis, dim):
    length = lax.axis_size(axis)
    blocks = lax.all_to_all(split_up(value, dim, length), axis, 0, 0, tiled=True)
    return jnp.sum(blocks, axis=0)


def filled_with(value, identity):
    return jax.tree.map(
        lambda a, e: jnp.broadcast_to(jnp.asarray(e, a.dtype), a.shape), value, identity
    )


def gathered_once(value, axis):
    leaves = jax.tree.leaves(value)
    sequence = sorted(range(len(leaves)), key=lambda k: -leaves[k].size)
    width = (1, *leaves[sequence[0]].shape)[-1]
    lines = [
        jnp.pad(leaves[k].reshape(-1), (0, -leaves[k].size % width)).reshape(-1, width)
        for k in sequence
    ]
    both, at, found = (lax.all_gather(jnp.concatenate(lines), axis), 0, {})
    for k, line in zip(sequence, lines):
        section = both[:, at : at + len(line)].reshape(len(both), -1)
        found[k] = section[:, : leaves[k].size].reshape(-1, *leaves[k].shape)
        at += len(line)
    numbers = iter(range(len(leaves)))
    return jax.tree.map(lambda _: found[next(numbers)], value)


def carried_in(value, axes, combine, identity):
    before = start = filled_with(value, identity)
    running = value
    for axis in reversed(axes):
        length, index = (lax.axis_size(axis), lax.axis_index(axis))
        pieces = gathered_once(running, axis)
        inside, running = (start, start)
        for k in range(length):
            passed = k < index
            running = combine(running, jax.tree.map(lambda part: part[k], pieces))
            inside = jax.tree.map(lambda new, old: jnp.where(passed, new, old), running, inside)
        before = combine(inside, before)
    return before


def shifted(value, axis, by):
    length = lax.axis_size(axis)
    pairs = [(i, i + by) for i in range(length) if 0 <= i + by < length]
    return lax.ppermute(value, axis, pairs)


def sum_at_owner(value, axis, dim):
    length = lax.axis_size(axis)
    blocks = lax.all_to_all(split_up(value, dim, length), axis, 0, 0, tiled=True)
    return jnp.sum(blocks.astype(jnp.float32), axis=0)


def silu_slope(values):
    sigmoid = jax.nn.sigmoid(values)
    return sigmoid * (1.0 + values * (1.0 - sigmoid))


def project(left, weight):
    return jnp.dot(left, weight, preferred_element_type=jnp.float32).astype(jnp.bfloat16)


def normalize(retrieved, norm_gain):
    mean_square = jnp.mean(retrieved * retrieved, axis=-1, keepdims=True)
    return (retrieved * lax.rsqrt(mean_square + epsilon) * norm_gain).astype(jnp.bfloat16)


def lookup(table, chosen):
    matches = jnp.arange(table.shape[0], dtype=jnp.int32)[:, None] == chosen
    return jnp.sum(jnp.where(matches, table, 0.0), axis=0)


def as_columns(vector):
    return vector[..., None, :]


def as_rows(vector):
    return vector[..., :, None]


def compose(earlier, later):
    (
        prior_decay,
        prior_cross,
        prior_keep,
        prior_speed_in,
        prior_speed_out,
        prior_weight_in,
        prior_weight_out,
    ) = earlier
    (
        after_decay,
        after_cross,
        after_keep,
        after_speed_in,
        after_speed_out,
        after_weight_in,
        after_weight_out,
    ) = later
    decay = after_decay * prior_decay
    cross = after_cross * prior_decay + after_keep * prior_cross
    keep = after_keep * prior_keep
    speed_in = as_columns(after_decay) * prior_speed_in + after_speed_in
    speed_out = as_rows(after_decay) * prior_speed_out + after_speed_out
    weight_in = (
        as_columns(after_cross) * prior_speed_in
        + as_columns(after_keep) * prior_weight_in
        + after_weight_in
    )
    weight_out = (
        as_rows(after_cross) * prior_speed_out
        + as_rows(after_keep) * prior_weight_out
        + after_weight_out
    )
    return (decay, cross, keep, speed_in, speed_out, weight_in, weight_out)


def window_attend(query, keys, values, block_index):
    query_count = query.shape[0]
    key_count = keys.shape[0]
    span_rows = key_count - query_count
    distance = (
        span_rows
        + jnp.arange(query_count, dtype=jnp.int32)[:, None]
        - jnp.arange(key_count, dtype=jnp.int32)[None, :]
    )
    key_pos = (block_index * query_count - span_rows + jnp.arange(key_count, dtype=jnp.int32))[
        None, :
    ]
    allowed = (distance >= 0) & (distance < span_rows) & (key_pos >= 0)
    contexts = []
    for head_number in range(query.shape[1] // HEAD_DIM):
        low_col = head_number * HEAD_DIM
        scores = jnp.einsum(
            "qd,kd->qk",
            query[:, low_col : low_col + HEAD_DIM],
            keys[:, low_col : low_col + HEAD_DIM],
            preferred_element_type=jnp.float32,
        ) * HEAD_DIM ** (-0.5)
        scores = jnp.where(allowed, scores, -1e30)
        row_peak = jnp.max(scores, axis=-1, keepdims=True)
        weights = jnp.exp(scores - row_peak)
        probabilities = (weights / jnp.sum(weights, axis=-1, keepdims=True)).astype(jnp.bfloat16)
        contexts.append(
            jnp.dot(
                probabilities,
                values[:, low_col : low_col + HEAD_DIM],
                preferred_element_type=jnp.float32,
            ).astype(jnp.bfloat16)
        )
    return jnp.concatenate(contexts, axis=1)


def shards(
    tokens,
    mem_query_w,
    mem_key_w,
    mem_value_w,
    mem_in,
    mem_out,
    forget_levels,
    momentum_levels,
    step_levels,
    plan,
    norm_gain,
    attn_query_w,
    attn_key_w,
    attn_value_w,
    attn_out_w,
):
    tok_rows = tokens.shape[0]
    share_rows = tok_rows // lax.axis_size("head")
    my_start = lax.axis_index("head") * share_rows
    mem_query, mem_key, mem_value = (
        lax.all_gather(project(tokens, mem_query_w), "head", axis=1, tiled=True),
        lax.all_gather(project(tokens, mem_key_w), "head", axis=1, tiled=True),
        lax.all_gather(project(tokens, mem_value_w), "head", axis=1, tiled=True),
    )
    keys_wide = mem_key.astype(jnp.float32)
    pre_act = jnp.dot(keys_wide, mem_in)
    hidden = jax.nn.silu(pre_act)
    predicted = sent_and_summed(jnp.dot(hidden, mem_out), "head", 0)
    value_share = lax.dynamic_slice_in_dim(mem_value, my_start, share_rows, 0).astype(jnp.float32)
    residual_err = lax.all_gather(
        2.0 / tok_rows * (predicted - value_share), "head", axis=0, tiled=True
    )
    grad_out = jnp.dot(hidden.T, residual_err)
    slope_term = jnp.dot(residual_err, mem_out.T) * silu_slope(pre_act)
    grad_in = jnp.dot(keys_wide.T, slope_term)
    chosen = plan[0]
    forget = lookup(forget_levels, chosen)
    momentum = lookup(momentum_levels, chosen)
    step_rate = lookup(step_levels, chosen)
    change_in = -as_columns(step_rate) * grad_in
    change_out = -as_rows(step_rate) * grad_out
    element = (momentum, momentum, 1.0 - forget, change_in, change_out, change_in, change_out)
    identity = (
        jnp.ones_like(momentum),
        jnp.zeros_like(momentum),
        jnp.ones_like(momentum),
        jnp.zeros_like(grad_in),
        jnp.zeros_like(grad_out),
        jnp.zeros_like(grad_in),
        jnp.zeros_like(grad_out),
    )
    entering = carried_in(element, SEQ, compose, identity)
    weight_in = as_columns(entering[2]) * mem_in + entering[5]
    weight_out = as_rows(entering[2]) * mem_out + entering[6]
    query_hidden = jax.nn.silu(jnp.dot(mem_query.astype(jnp.float32), weight_in))
    retrieved = sent_and_summed(jnp.dot(query_hidden, weight_out), "head", 0)
    normed = lax.all_gather(normalize(retrieved, norm_gain), "head", axis=0, tiled=True)
    att_query = project(normed, attn_query_w)
    att_key = project(normed, attn_key_w)
    att_value = project(normed, attn_value_w)
    earlier = []
    for distance in range(SPAN, 0, -1):
        earlier.append(shifted((att_key, att_value), SEQ, distance))
    key_window = jnp.concatenate([received[0] for received in earlier] + [att_key], axis=0)
    value_window = jnp.concatenate([received[1] for received in earlier] + [att_value], axis=0)
    context = window_attend(att_query, key_window, value_window, lax.axis_index(SEQ))
    partial_out = jnp.dot(context, attn_out_w, preferred_element_type=jnp.float32)
    return sum_at_owner(partial_out.astype(jnp.bfloat16), "head", 1).astype(jnp.bfloat16)


def solution(mesh):
    split = Mesh(
        mesh.devices.reshape(4, 4, 2, mesh.shape["head"]), ("seq_0", "seq_1", "seq_2", "head")
    )
    in_specs = (
        P(SEQ, None),
        P(None, "head"),
        P(None, "head"),
        P(None, "head"),
        P(None, "head"),
        P("head", None),
        P(None, "head"),
        P(None, "head"),
        P(None, "head"),
        P(SEQ),
        P(),
        P(None, "head"),
        P(None, "head"),
        P(None, "head"),
        P("head", None),
    )
    out_specs = P(SEQ, "head")
    return jax.shard_map(
        shards, mesh=split, in_specs=in_specs, out_specs=out_specs, check_vma=False
    )
```

profile of v0, /device:TPU:33, one launch (start us, length us, event | category | flops | bytes accessed | tf_op | source)
XLA Modules:
  0.0 816.8 jit_solution(12139986413345933075)
XLA Ops:
  9.8 61.9 %all-gather.17.cloned.1.call-done = bf16[512,1024]{1,0:T(8,128)(2,1)} async-done(((bf16[512,128]{1,0:T(8,128)(2,1)}), bf16[512,1024]{1,0:T(8,128)(2,1)}) %all-gather.17.cloned.1.call-update) | async-done | bytes 1048592 | tf_op jit(solution)/shard_map/all_gather | solution.py:196
  76.0 3.7 all-to-all-start
  81.0 54.1 %all-to-all-done = f32[8,64,1024]{2,1,0:T(8,128)S(1)} async-done(((f32[8,64,1024]{2,1,0:T(8,128)}), f32[8,64,1024]{2,1,0:T(8,128)S(1)}, u32[]{:S(2)}, u32[]{:S(2)}) %all-to-all-start) | async-done | bytes 2097184 | tf_op jit(solution)/shard_map/all_to_all | solution.py:20
  135.3 23.0 %all-gather.19.cloned.1.call-done = bf16[512,1024]{1,0:T(8,128)(2,1)} async-done(((bf16[512,128]{1,0:T(8,128)(2,1)}), bf16[512,1024]{1,0:T(8,128)(2,1)}) %all-gather.19.cloned.1.call-update) | async-done | bytes 1048592 | tf_op jit(solution)/shard_map/all_gather | solution.py:197
  160.7 57.5 %all-gather.21.cloned.1.call-done = bf16[512,1024]{1,0:T(8,128)(2,1)} async-done(((bf16[64,1024]{1,0:T(8,128)(2,1)}), bf16[512,1024]{1,0:T(8,128)(2,1)}) %all-gather.21.cloned.1.call-update) | async-done | bytes 1048592 | tf_op jit(solution)/shard_map/all_gather | solution.py:204
  220.0 2.6 convolution_multiply_fusion
  222.7 4.1 concatenate.18
  226.8 17.6 %all-gather.25.cloned.1.call-done = f32[2,4099,128]{2,1,0:T(8,128)} async-done(((f32[1,4099,128]{2,1,0:T(8,128)}), f32[2,4099,128]{2,1,0:T(8,128)}) %all-gather.25.cloned.1.call-update) | async-done | bytes 4197392 | tf_op jit(solution)/shard_map/all_gather | solution.py:38
  251.5 4.1 concatenate.19
  255.6 154.2 %all-gather.27.cloned.1.call-done = f32[4,4099,128]{2,1,0:T(8,128)} async-done(((f32[1,4099,128]{2,1,0:T(8,128)}), f32[4,4099,128]{2,1,0:T(8,128)}) %all-gather.27.cloned.1.call-update) | async-done | bytes 8394768 | tf_op jit(solution)/shard_map/all_gather | solution.py:38
  418.9 4.0 bitcast_add_fusion
  423.0 4.1 concatenate.20
  433.9 3.4 fusion.353
  446.6 65.9 %all-gather.29.cloned.1.call-done = f32[4,4099,128]{2,1,0:T(8,128)} async-done(((f32[1,4099,128]{2,1,0:T(8,128)}), f32[4,4099,128]{2,1,0:T(8,128)}) %all-gather.29.cloned.1.call-update) | async-done | bytes 8394768 | tf_op jit(solution)/shard_map/all_gather | solution.py:38
  512.5 3.4 fusion.352
  526.8 48.5 %all-gather.15.cloned.1.call-done = bf16[512,1024]{1,0:T(8,128)(2,1)} async-done(((bf16[512,128]{1,0:T(8,128)(2,1)}), bf16[512,1024]{1,0:T(8,128)(2,1)}) %all-gather.15.cloned.1.call-update) | async-done | bytes 1048592 | tf_op jit(solution)/shard_map/all_gather | solution.py:195
  575.3 11.3 %fusion.57 = f32[512,1024]{1,0:T(8,128)} fusion(f32[128,1024]{1,0:T(8,128)} %squeeze.275, f32[128,1024]{1,0:T(8,128)} %squeeze.274, f32[128,1024]{1,0:T(8,128)} %squeeze.273, f32[128,1024]{1,0:T(8,128)} %squeeze.272, f32[128,1024]{1,0:T(8,128)} %squeeze.271, f32[128,1024]{1,0:T(8,128)} %squeeze.270, f32[128,1024]{1,0:T(8,128)} %squeeze.269, ...), kind=kOutput, calls=%fused_computation.101 | convolution fusion | flops 287834112 | bytes 25205248 | tf_op jit(solution)/shard_map/dot_general | solution.py:230
  586.6 56.2 %all_to_all.15 = f32[8,64,1024]{2,1,0:T(8,128)S(1)} all-to-all(f32[8,64,1024]{2,1,0:T(8,128)} %bitcast.561), channel_id=1, replica_groups=mesh['seq_0'=4,'seq_1'=4,'seq_2'=2,'head'=8] {'head'}, dimensions={0} | all-to-all | bytes 4194304 | tf_op jit(solution)/shard_map/all_to_all | solution.py:20
  644.3 54.3 %all-gather.23.cloned.1.call-done = bf16[512,1024]{1,0:T(8,128)(2,1)} async-done(((bf16[64,1024]{1,0:T(8,128)(2,1)}), bf16[512,1024]{1,0:T(8,128)(2,1)}) %all-gather.23.cloned.1.call-update) | async-done | bytes 1048592 | tf_op jit(solution)/shard_map/all_gather | solution.py:231
  700.3 3.1 collective-permute-start
  703.5 5.4 collective-permute-start.1
  708.9 3.6 collective-permute-start.2
  713.8 4.1 collective-permute-start.4
  720.1 3.0 collective-permute-start.5
  725.4 3.3 collective-permute-start.7
  731.5 8.3 %collective-permute-start.10 = (bf16[512,128]{1,0:T(8,128)(2,1)S(1)}, bf16[512,128]{1,0:T(8,128)(2,1)S(1)}, u32[]{:S(2)}, u32[]{:S(2)}) collective-permute-start(bf16[512,128]{1,0:T(8,128)(2,1)S(1)} %convolution_convert_fusion.1), channel_id=1, source_target_pairs={{0,48},{8,56},{16,64},{24,72},{32,80},{40,88},{48,96},{56,104},{64... | collective-permute-start | bytes 393224 | tf_op jit(solution)/shard_map/ppermute | solution.py:65
  739.8 2.8 collective-permute-start.11
  744.2 4.3 fusion.356
  748.5 4.2 fusion.355
  752.7 4.3 collective-permute-start.13
  759.1 3.0 collective-permute-start.15
  773.0 36.1 %all_to_all.16 = bf16[8,512,128]{2,1,0:T(8,128)(2,1)S(1)} all-to-all(bf16[8,512,128]{2,1,0:T(8,128)(2,1)S(1)} %bitcast.560), channel_id=1, replica_groups=mesh['seq_0'=4,'seq_1'=4,'seq_2'=2,'head'=8] {'head'}, dimensions={0} | all-to-all | bytes 2097152 | tf_op jit(solution)/shard_map/all_to_all | solution.py:70
  (202 shorter events, 82.1 us)
Async XLA Ops:
  6.5 67.7 %copy-start.14 = (f32[128,1024]{1,0:T(8,128)S(1)}, f32[128,1024]{1,0:T(8,128)}, u32[]{:S(2)}) copy-start(f32[128,1024]{1,0:T(8,128)} %param.20) | copy-start | bytes 1572868
  6.5 65.2 %all-gather.17.cloned.1.call-start = ((), (), s32[]{:S(2)}) async-start(), calls=%async_computation.4 | async-start | bytes 1179648 | tf_op jit(solution)/shard_map/all_gather | solution.py:196
  76.0 59.1 %all-to-all-start = ((f32[8,64,1024]{2,1,0:T(8,128)}), f32[8,64,1024]{2,1,0:T(8,128)S(1)}, u32[]{:S(2)}, u32[]{:S(2)}) async-start(f32[8,64,1024]{2,1,0:T(8,128)} %bitcast.559), calls=%async_computation | async-start | bytes 4194304 | tf_op jit(solution)/shard_map/all_to_all | solution.py:20
  79.7 80.9 %copy-start.21 = (f32[16,128]{1,0:T(8,128)S(1)}, f32[16,128]{1,0:T(8,128)}, u32[]{:S(2)}) copy-start(f32[16,128]{1,0:T(8,128)} %param.21) | copy-start | bytes 24580
  79.7 80.9 %copy-start.22 = (f32[16,128]{1,0:T(8,128)S(1)}, f32[16,128]{1,0:T(8,128)}, u32[]{:S(2)}) copy-start(f32[16,128]{1,0:T(8,128)} %param.22) | copy-start | bytes 24580
  79.7 80.9 %copy-start.23 = (f32[16,128]{1,0:T(8,128)S(1)}, f32[16,128]{1,0:T(8,128)}, u32[]{:S(2)}) copy-start(f32[16,128]{1,0:T(8,128)} %param.23) | copy-start | bytes 24580
  79.8 78.5 %all-gather.19.cloned.1.call-start = ((), (), s32[]{:S(2)}) async-start(), calls=%async_computation.5 | async-start | bytes 1179648 | tf_op jit(solution)/shard_map/all_gather | solution.py:197
  80.9 137.3 %all-gather.21.cloned.1.call-start = ((), (), s32[]{:S(2)}) async-start(), calls=%async_computation.6 | async-start | bytes 1179648 | tf_op jit(solution)/shard_map/all_gather | solution.py:204
  135.2 84.8 %copy-start.11 = (bf16[512,1024]{1,0:T(8,128)(2,1)S(1)}, bf16[512,1024]{1,0:T(8,128)(2,1)}, u32[]{:S(2)}) copy-start(bf16[512,1024]{1,0:T(8,128)(2,1)} %all-gather.17.cloned.1.call-done) | copy-start | bytes 3145732
  159.8 84.5 %all-gather.25.cloned.1.call-start = ((), (), s32[]{:S(2)}) async-start(), calls=%async_computation.8 | async-start | bytes 6303744 | tf_op jit(solution)/shard_map/all_gather | solution.py:38
  226.8 183.1 %all-gather.27.cloned.1.call-start = ((), (), s32[]{:S(2)}) async-start(), calls=%async_computation.9 | async-start | bytes 10506240 | tf_op jit(solution)/shard_map/all_gather | solution.py:38
  255.6 256.9 %all-gather.29.cloned.1.call-start = ((), (), s32[]{:S(2)}) async-start(), calls=%async_computation.10 | async-start | bytes 10506240 | tf_op jit(solution)/shard_map/all_gather | solution.py:38
  427.1 148.2 %all-gather.15.cloned.1.call-start = ((), (), s32[]{:S(2)}) async-start(), calls=%async_computation.3 | async-start | bytes 1179648 | tf_op jit(solution)/shard_map/all_gather | solution.py:195
  428.3 270.3 %all-gather.23.cloned.1.call-start = ((), (), s32[]{:S(2)}) async-start(), calls=%async_computation.7 | async-start | bytes 1179648 | tf_op jit(solution)/shard_map/all_gather | solution.py:231
  643.0 74.9 %copy-start.18 = (bf16[1024,128]{1,0:T(8,128)(2,1)S(1)}, bf16[1024,128]{1,0:T(8,128)(2,1)}, u32[]{:S(2)}) copy-start(bf16[1024,128]{1,0:T(8,128)(2,1)} %param.26) | copy-start | bytes 786436
  643.0 76.6 %copy-start.19 = (bf16[1024,128]{1,0:T(8,128)(2,1)S(1)}, bf16[1024,128]{1,0:T(8,128)(2,1)}, u32[]{:S(2)}) copy-start(bf16[1024,128]{1,0:T(8,128)(2,1)} %param.28) | copy-start | bytes 786436
  700.3 19.7 %collective-permute-start = (bf16[512,128]{1,0:T(8,128)(2,1)S(1)}, bf16[512,128]{1,0:T(8,128)(2,1)S(1)}, u32[]{:S(2)}, u32[]{:S(2)}) collective-permute-start(bf16[512,128]{1,0:T(8,128)(2,1)S(1)} %convolution_convert_fusion.2), channel_id=1, source_target_pairs={{0,64},{8,72},{16,80},{24,88},{32,96},{40,104},{48,112},{56,120},{... | collective-permute-start | bytes 393224 | tf_op jit(solution)/shard_map/ppermute | solution.py:65
  703.5 19.7 %collective-permute-start.1 = (bf16[512,128]{1,0:T(8,128)(2,1)S(1)}, bf16[512,128]{1,0:T(8,128)(2,1)S(1)}, u32[]{:S(2)}, u32[]{:S(2)}) collective-permute-start(bf16[512,128]{1,0:T(8,128)(2,1)S(1)} %convolution_convert_fusion.2), channel_id=1, source_target_pairs={{0,56},{8,64},{16,72},{24,80},{32,88},{40,96},{48,104},{56,112},{6... | collective-permute-start | bytes 393224 | tf_op jit(solution)/shard_map/ppermute | solution.py:65
  708.9 16.6 %collective-permute-start.2 = (bf16[512,128]{1,0:T(8,128)(2,1)S(1)}, bf16[512,128]{1,0:T(8,128)(2,1)S(1)}, u32[]{:S(2)}, u32[]{:S(2)}) collective-permute-start(bf16[512,128]{1,0:T(8,128)(2,1)S(1)} %convolution_convert_fusion.2), channel_id=1, source_target_pairs={{0,48},{8,56},{16,64},{24,72},{32,80},{40,88},{48,96},{56,104},{64... | collective-permute-start | bytes 393224 | tf_op jit(solution)/shard_map/ppermute | solution.py:65
  712.5 16.3 %collective-permute-start.3 = (bf16[512,128]{1,0:T(8,128)(2,1)S(1)}, bf16[512,128]{1,0:T(8,128)(2,1)S(1)}, u32[]{:S(2)}, u32[]{:S(2)}) collective-permute-start(bf16[512,128]{1,0:T(8,128)(2,1)S(1)} %convolution_convert_fusion.2), channel_id=1, source_target_pairs={{0,40},{8,48},{16,56},{24,64},{32,72},{40,80},{48,88},{56,96},{64,... | collective-permute-start | bytes 393224 | tf_op jit(solution)/shard_map/ppermute | solution.py:65
  713.8 16.3 %collective-permute-start.4 = (bf16[512,128]{1,0:T(8,128)(2,1)S(1)}, bf16[512,128]{1,0:T(8,128)(2,1)S(1)}, u32[]{:S(2)}, u32[]{:S(2)}) collective-permute-start(bf16[512,128]{1,0:T(8,128)(2,1)S(1)} %convolution_convert_fusion.2), channel_id=1, source_target_pairs={{0,32},{8,40},{16,48},{24,56},{32,64},{40,72},{48,80},{56,88},{64,... | collective-permute-start | bytes 393224 | tf_op jit(solution)/shard_map/ppermute | solution.py:65
  720.1 11.4 %collective-permute-start.5 = (bf16[512,128]{1,0:T(8,128)(2,1)S(1)}, bf16[512,128]{1,0:T(8,128)(2,1)S(1)}, u32[]{:S(2)}, u32[]{:S(2)}) collective-permute-start(bf16[512,128]{1,0:T(8,128)(2,1)S(1)} %convolution_convert_fusion.2), channel_id=1, source_target_pairs={{0,24},{8,32},{16,40},{24,48},{32,56},{40,64},{48,72},{56,80},{64,... | collective-permute-start | bytes 393224 | tf_op jit(solution)/shard_map/ppermute | solution.py:65
  723.1 16.6 %collective-permute-start.6 = (bf16[512,128]{1,0:T(8,128)(2,1)S(1)}, bf16[512,128]{1,0:T(8,128)(2,1)S(1)}, u32[]{:S(2)}, u32[]{:S(2)}) collective-permute-start(bf16[512,128]{1,0:T(8,128)(2,1)S(1)} %convolution_convert_fusion.2), channel_id=1, source_target_pairs={{0,16},{8,24},{16,32},{24,40},{32,48},{40,56},{48,64},{56,72},{64,... | collective-permute-start | bytes 393224 | tf_op jit(solution)/shard_map/ppermute | solution.py:65
  725.4 17.1 %collective-permute-start.7 = (bf16[512,128]{1,0:T(8,128)(2,1)S(1)}, bf16[512,128]{1,0:T(8,128)(2,1)S(1)}, u32[]{:S(2)}, u32[]{:S(2)}) collective-permute-start(bf16[512,128]{1,0:T(8,128)(2,1)S(1)} %convolution_convert_fusion.2), channel_id=1, source_target_pairs={{0,8},{8,16},{16,24},{24,32},{32,40},{40,48},{48,56},{56,64},{64,7... | collective-permute-start | bytes 393224 | tf_op jit(solution)/shard_map/ppermute | solution.py:65
  728.8 23.9 %collective-permute-start.8 = (bf16[512,128]{1,0:T(8,128)(2,1)S(1)}, bf16[512,128]{1,0:T(8,128)(2,1)S(1)}, u32[]{:S(2)}, u32[]{:S(2)}) collective-permute-start(bf16[512,128]{1,0:T(8,128)(2,1)S(1)} %convolution_convert_fusion.1), channel_id=1, source_target_pairs={{0,64},{8,72},{16,80},{24,88},{32,96},{40,104},{48,112},{56,120},{... | collective-permute-start | bytes 393224 | tf_op jit(solution)/shard_map/ppermute | solution.py:65
  730.1 26.9 %collective-permute-start.9 = (bf16[512,128]{1,0:T(8,128)(2,1)S(1)}, bf16[512,128]{1,0:T(8,128)(2,1)S(1)}, u32[]{:S(2)}, u32[]{:S(2)}) collective-permute-start(bf16[512,128]{1,0:T(8,128)(2,1)S(1)} %convolution_convert_fusion.1), channel_id=1, source_target_pairs={{0,56},{8,64},{16,72},{24,80},{32,88},{40,96},{48,104},{56,112},{6... | collective-permute-start | bytes 393224 | tf_op jit(solution)/shard_map/ppermute | solution.py:65
  731.5 27.6 %collective-permute-start.10 = (bf16[512,128]{1,0:T(8,128)(2,1)S(1)}, bf16[512,128]{1,0:T(8,128)(2,1)S(1)}, u32[]{:S(2)}, u32[]{:S(2)}) collective-permute-start(bf16[512,128]{1,0:T(8,128)(2,1)S(1)} %convolution_convert_fusion.1), channel_id=1, source_target_pairs={{0,48},{8,56},{16,64},{24,72},{32,80},{40,88},{48,96},{56,104},{64... | collective-permute-start | bytes 393224 | tf_op jit(solution)/shard_map/ppermute | solution.py:65
  739.8 22.3 %collective-permute-start.11 = (bf16[512,128]{1,0:T(8,128)(2,1)S(1)}, bf16[512,128]{1,0:T(8,128)(2,1)S(1)}, u32[]{:S(2)}, u32[]{:S(2)}) collective-permute-start(bf16[512,128]{1,0:T(8,128)(2,1)S(1)} %convolution_convert_fusion.1), channel_id=1, source_target_pairs={{0,40},{8,48},{16,56},{24,64},{32,72},{40,80},{48,88},{56,96},{64,... | collective-permute-start | bytes 393224 | tf_op jit(solution)/shard_map/ppermute | solution.py:65
  742.6 19.6 %collective-permute-start.12 = (bf16[512,128]{1,0:T(8,128)(2,1)S(1)}, bf16[512,128]{1,0:T(8,128)(2,1)S(1)}, u32[]{:S(2)}, u32[]{:S(2)}) collective-permute-start(bf16[512,128]{1,0:T(8,128)(2,1)S(1)} %convolution_convert_fusion.1), channel_id=1, source_target_pairs={{0,32},{8,40},{16,48},{24,56},{32,64},{40,72},{48,80},{56,88},{64,... | collective-permute-start | bytes 393224 | tf_op jit(solution)/shard_map/ppermute | solution.py:65
  752.7 9.5 %collective-permute-start.13 = (bf16[512,128]{1,0:T(8,128)(2,1)S(1)}, bf16[512,128]{1,0:T(8,128)(2,1)S(1)}, u32[]{:S(2)}, u32[]{:S(2)}) collective-permute-start(bf16[512,128]{1,0:T(8,128)(2,1)S(1)} %convolution_convert_fusion.1), channel_id=1, source_target_pairs={{0,24},{8,32},{16,40},{24,48},{32,56},{40,64},{48,72},{56,80},{64,... | collective-permute-start | bytes 393224 | tf_op jit(solution)/shard_map/ppermute | solution.py:65
  757.1 6.9 collective-permute-start.14
  759.1 6.2 collective-permute-start.15
  (18 other events, 380.4 us)
Sparse Core Ops, SparseCore 0:
  9.9 61.7 all-gather.16
  83.1 75.1 all-gather.18
  160.9 57.3 all-gather.20
  226.9 17.4 all-gather.24
  255.7 154.1 all-gather.26
  427.3 85.1 all-gather.28
  515.0 60.2 all-gather.14
  644.4 54.1 all-gather.22
where the time goes:
time: 818 us; the launch traced here: 817 us
  waiting for transfers between devices  540 us (66%)
  blocking collectives  92.3 us (11%)
  starting transfers between devices  54.7 us (7%)
  local copies, waits for them, and re-layouts  47.1 us (6%)
  matrix products  40.3 us (5%)
  other arithmetic  27 us (3%)
  between operations  15.1 us (2%)
    all_gather x3, waiting for transfers between devices, gathered_once(): both, at, found = (lax.all_gather(jnp.concatenate(lines), axis), 0, {})  238 us
    all_gather x1, waiting for transfers between devices, shards(): lax.all_gather(project(tokens, mem_key_w), 'head', axis=1, tiled=True)  61.9 us
    all_gather x1, waiting for transfers between devices, shards(): lax.all_gather(2.0 / tok_rows * (predicted - value_share), 'head', axis=0...  57.5 us
    all_to_all x1, blocking collectives, sent_and_summed(): lax.all_to_all(split_up(value, dim, length), axis, 0, 0, tiled=True)  56.2 us
    all_gather x1, waiting for transfers between devices, shards(): lax.all_gather(normalize(retrieved, norm_gain), 'head', axis=0, tiled=True)  54.3 us
    all_to_all x1, waiting for transfers between devices, sent_and_summed(): lax.all_to_all(split_up(value, dim, length), axis, 0, 0, tiled=True)  54.1 us
    ppermute x16, starting transfers between devices, shifted(): return lax.ppermute(value, axis, pairs)  50.5 us
    all_gather x1, waiting for transfers between devices, shards(): lax.all_gather(project(tokens, mem_query_w), 'head', axis=1, tiled=True)  48.5 us
  transfers between devices with their start and end apart: 25, of which 11 were waited for; matrix products, arithmetic and copies ran while one was open for 6% of the time, Pallas kernels for 0%

commit v1 on v0

--- a/solution.py
+++ b/solution.py
@@ -228,7 +228,12 @@
     weight_out = as_rows(entering[2]) * mem_out + entering[6]
     query_hidden = jax.nn.silu(jnp.dot(mem_query.astype(jnp.float32), weight_in))
     retrieved = sent_and_summed(jnp.dot(query_hidden, weight_out), "head", 0)
-    normed = lax.all_gather(normalize(retrieved, norm_gain), "head", axis=0, tiled=True)
+    normed = jnp.concatenate(
+        lax.all_to_all(
+            jnp.stack([normalize(retrieved, norm_gain)] * lax.axis_size("head")), "head", 0, 0
+        ),
+        axis=0,
+    )
     att_query = project(normed, attn_query_w)
     att_key = project(normed, attn_key_w)
     att_value = project(normed, attn_value_w)

time: 818 us -> 788 us (0.963)
  waiting for transfers between devices: 540 us -> 508 us
    all_gather x1 -> x0, waiting for transfers between devices: 54.3 us -> none  [shards(): lax.all_gather(normalize(retrieved, norm_gain), 'head', axis=0, tiled=True)]
    all_to_all x0 -> x1, waiting for transfers between devices: none -> 23.7 us  [shards(): lax.all_to_all(jnp.stack([normalize(retrieved, norm_gain)] * lax.axis_siz...]
where the time goes in v1:
time: 788 us; the launch traced here: 786 us
  waiting for transfers between devices  508 us (64%)
  blocking collectives  90 us (11%)
  starting transfers between devices  60.3 us (8%)
  local copies, waits for them, and re-layouts  48.2 us (6%)
  matrix products  37.8 us (5%)
  other arithmetic  26.4 us (3%)
  between operations  15.1 us (2%)
    all_gather x3, waiting for transfers between devices, gathered_once(): both, at, found = (lax.all_gather(jnp.concatenate(lines), axis), 0, {})  238 us
    all_gather x1, waiting for transfers between devices, shards(): lax.all_gather(project(tokens, mem_key_w), 'head', axis=1, tiled=True)  61.9 us
    all_gather x1, waiting for transfers between devices, shards(): lax.all_gather(2.0 / tok_rows * (predicted - value_share), 'head', axis=0...  57.5 us
    all_to_all x1, blocking collectives, sent_and_summed(): lax.all_to_all(split_up(value, dim, length), axis, 0, 0, tiled=True)  56.4 us
    all_to_all x1, waiting for transfers between devices, sent_and_summed(): lax.all_to_all(split_up(value, dim, length), axis, 0, 0, tiled=True)  54.1 us
    ppermute x16, starting transfers between devices, shifted(): return lax.ppermute(value, axis, pairs)  52.4 us
    all_gather x1, waiting for transfers between devices, shards(): lax.all_gather(project(tokens, mem_query_w), 'head', axis=1, tiled=True)  48.6 us
    all_to_all x1, blocking collectives, sum_at_owner(): lax.all_to_all(split_up(value, dim, length), axis, 0, 0, tiled=True)  33.6 us
  transfers between devices with their start and end apart: 25, of which 11 were waited for; matrix products, arithmetic and copies ran while one was open for 6% of the time, Pallas kernels for 0%

profile of v1, /device:TPU:33, one launch (start us, length us, event | category | flops | bytes accessed | tf_op | source)
XLA Modules:
  0.0 786.0 jit_solution(1972052235393403069)
XLA Ops:
  9.8 61.9 %all-gather.16.cloned.1.call-done = bf16[512,1024]{1,0:T(8,128)(2,1)} async-done(((bf16[512,128]{1,0:T(8,128)(2,1)}), bf16[512,1024]{1,0:T(8,128)(2,1)}) %all-gather.16.cloned.1.call-update) | async-done | bytes 1048592 | tf_op jit(solution)/shard_map/all_gather | solution.py:196
  76.0 3.7 all-to-all-start
  81.0 54.1 %all-to-all-done = f32[8,64,1024]{2,1,0:T(8,128)S(1)} async-done(((f32[8,64,1024]{2,1,0:T(8,128)}), f32[8,64,1024]{2,1,0:T(8,128)S(1)}, u32[]{:S(2)}, u32[]{:S(2)}) %all-to-all-start) | async-done | bytes 2097184 | tf_op jit(solution)/shard_map/all_to_all | solution.py:20
  135.3 23.0 %all-gather.18.cloned.1.call-done = bf16[512,1024]{1,0:T(8,128)(2,1)} async-done(((bf16[512,128]{1,0:T(8,128)(2,1)}), bf16[512,1024]{1,0:T(8,128)(2,1)}) %all-gather.18.cloned.1.call-update) | async-done | bytes 1048592 | tf_op jit(solution)/shard_map/all_gather | solution.py:197
  160.7 57.5 %all-gather.20.cloned.1.call-done = bf16[512,1024]{1,0:T(8,128)(2,1)} async-done(((bf16[64,1024]{1,0:T(8,128)(2,1)}), bf16[512,1024]{1,0:T(8,128)(2,1)}) %all-gather.20.cloned.1.call-update) | async-done | bytes 1048592 | tf_op jit(solution)/shard_map/all_gather | solution.py:204
  222.7 4.1 concatenate.18
  226.9 17.6 %all-gather.22.cloned.1.call-done = f32[2,4099,128]{2,1,0:T(8,128)} async-done(((f32[1,4099,128]{2,1,0:T(8,128)}), f32[2,4099,128]{2,1,0:T(8,128)}) %all-gather.22.cloned.1.call-update) | async-done | bytes 4197392 | tf_op jit(solution)/shard_map/all_gather | solution.py:38
  251.5 4.1 concatenate.19
  255.7 154.2 %all-gather.24.cloned.1.call-done = f32[4,4099,128]{2,1,0:T(8,128)} async-done(((f32[1,4099,128]{2,1,0:T(8,128)}), f32[4,4099,128]{2,1,0:T(8,128)}) %all-gather.24.cloned.1.call-update) | async-done | bytes 8394768 | tf_op jit(solution)/shard_map/all_gather | solution.py:38
  419.0 4.0 bitcast_add_fusion
  423.1 4.1 concatenate.20
  433.9 3.4 fusion.353
  446.6 65.9 %all-gather.26.cloned.1.call-done = f32[4,4099,128]{2,1,0:T(8,128)} async-done(((f32[1,4099,128]{2,1,0:T(8,128)}), f32[4,4099,128]{2,1,0:T(8,128)}) %all-gather.26.cloned.1.call-update) | async-done | bytes 8394768 | tf_op jit(solution)/shard_map/all_gather | solution.py:38
  512.6 3.4 fusion.352
  526.8 48.6 %all-gather.14.cloned.1.call-done = bf16[512,1024]{1,0:T(8,128)(2,1)} async-done(((bf16[512,128]{1,0:T(8,128)(2,1)}), bf16[512,1024]{1,0:T(8,128)(2,1)}) %all-gather.14.cloned.1.call-update) | async-done | bytes 1048592 | tf_op jit(solution)/shard_map/all_gather | solution.py:195
  575.4 11.3 %fusion.57 = f32[512,1024]{1,0:T(8,128)} fusion(f32[128,1024]{1,0:T(8,128)} %squeeze.275, f32[128,1024]{1,0:T(8,128)} %squeeze.274, f32[128,1024]{1,0:T(8,128)} %squeeze.273, f32[128,1024]{1,0:T(8,128)} %squeeze.272, f32[128,1024]{1,0:T(8,128)} %squeeze.271, f32[128,1024]{1,0:T(8,128)} %squeeze.270, f32[128,1024]{1,0:T(8,128)} %squeeze.269, ...), kind=kOutput, calls=%fused_computation.101 | convolution fusion | flops 287834112 | bytes 25205248 | tf_op jit(solution)/shard_map/dot_general | solution.py:230
  586.7 56.4 %all_to_all.20 = f32[8,64,1024]{2,1,0:T(8,128)S(1)} all-to-all(f32[8,64,1024]{2,1,0:T(8,128)} %bitcast.565), channel_id=1, replica_groups=mesh['seq_0'=4,'seq_1'=4,'seq_2'=2,'head'=8] {'head'}, dimensions={0} | all-to-all | bytes 4194304 | tf_op jit(solution)/shard_map/all_to_all | solution.py:20
  645.0 3.7 all-to-all-start.2
  648.7 23.7 %all-to-all-done.2 = bf16[8,64,1024]{2,1,0:T(8,128)(2,1)S(1)} async-done(((bf16[8,64,1024]{2,1,0:T(8,128)(2,1)}), bf16[8,64,1024]{2,1,0:T(8,128)(2,1)S(1)}, u32[]{:S(2)}, u32[]{:S(2)}) %all-to-all-start.2) | async-done | bytes 1048608 | tf_op jit(solution)/shard_map/all_to_all | solution.py:232
  672.9 3.1 collective-permute-start
  676.0 3.8 collective-permute-start.1
  681.1 6.3 collective-permute-start.3
  689.7 3.6 collective-permute-start.5
  695.7 3.7 collective-permute-start.7
  702.6 8.9 %collective-permute-start.10 = (bf16[512,128]{1,0:T(8,128)(2,1)S(1)}, bf16[512,128]{1,0:T(8,128)(2,1)S(1)}, u32[]{:S(2)}, u32[]{:S(2)}) collective-permute-start(bf16[512,128]{1,0:T(8,128)(2,1)S(1)} %convolution_convert_fusion.1), channel_id=1, source_target_pairs={{0,48},{8,56},{16,64},{24,72},{32,80},{40,88},{48,96},{56,104},{64... | collective-permute-start | bytes 393224 | tf_op jit(solution)/shard_map/ppermute | solution.py:65
  712.9 3.7 collective-permute-start.12
  716.7 4.3 fusion.356
  721.0 4.2 fusion.355
  725.2 3.6 collective-permute-start.13
  728.8 2.8 collective-permute-start.14
  731.7 3.6 collective-permute-start.15
  744.8 33.6 %all_to_all.21 = bf16[8,512,128]{2,1,0:T(8,128)(2,1)S(1)} all-to-all(bf16[8,512,128]{2,1,0:T(8,128)(2,1)S(1)} %bitcast.564), channel_id=1, replica_groups=mesh['seq_0'=4,'seq_1'=4,'seq_2'=2,'head'=8] {'head'}, dimensions={0} | all-to-all | bytes 2097152 | tf_op jit(solution)/shard_map/all_to_all | solution.py:70
  (200 shorter events, 81.1 us)
Async XLA Ops:
  6.5 67.7 %copy-start.13 = (f32[128,1024]{1,0:T(8,128)S(1)}, f32[128,1024]{1,0:T(8,128)}, u32[]{:S(2)}) copy-start(f32[128,1024]{1,0:T(8,128)} %param.20) | copy-start | bytes 1572868
  6.5 65.2 %all-gather.16.cloned.1.call-start = ((), (), s32[]{:S(2)}) async-start(), calls=%async_computation.5 | async-start | bytes 1179648 | tf_op jit(solution)/shard_map/all_gather | solution.py:196
  76.0 59.1 %all-to-all-start = ((f32[8,64,1024]{2,1,0:T(8,128)}), f32[8,64,1024]{2,1,0:T(8,128)S(1)}, u32[]{:S(2)}, u32[]{:S(2)}) async-start(f32[8,64,1024]{2,1,0:T(8,128)} %bitcast.563), calls=%async_computation | async-start | bytes 4194304 | tf_op jit(solution)/shard_map/all_to_all | solution.py:20
  79.7 80.9 %copy-start.20 = (f32[16,128]{1,0:T(8,128)S(1)}, f32[16,128]{1,0:T(8,128)}, u32[]{:S(2)}) copy-start(f32[16,128]{1,0:T(8,128)} %param.21) | copy-start | bytes 24580
  79.8 80.9 %copy-start.21 = (f32[16,128]{1,0:T(8,128)S(1)}, f32[16,128]{1,0:T(8,128)}, u32[]{:S(2)}) copy-start(f32[16,128]{1,0:T(8,128)} %param.22) | copy-start | bytes 24580
  79.8 80.9 %copy-start.22 = (f32[16,128]{1,0:T(8,128)S(1)}, f32[16,128]{1,0:T(8,128)}, u32[]{:S(2)}) copy-start(f32[16,128]{1,0:T(8,128)} %param.23) | copy-start | bytes 24580
  79.8 78.5 %all-gather.18.cloned.1.call-start = ((), (), s32[]{:S(2)}) async-start(), calls=%async_computation.6 | async-start | bytes 1179648 | tf_op jit(solution)/shard_map/all_gather | solution.py:197
  81.0 137.3 %all-gather.20.cloned.1.call-start = ((), (), s32[]{:S(2)}) async-start(), calls=%async_computation.7 | async-start | bytes 1179648 | tf_op jit(solution)/shard_map/all_gather | solution.py:204
  135.3 84.8 %copy-start.10 = (bf16[512,1024]{1,0:T(8,128)(2,1)S(1)}, bf16[512,1024]{1,0:T(8,128)(2,1)}, u32[]{:S(2)}) copy-start(bf16[512,1024]{1,0:T(8,128)(2,1)} %all-gather.16.cloned.1.call-done) | copy-start | bytes 3145732
  159.8 60.2 %copy-start.12 = (f32[512,128]{1,0:T(8,128)S(1)}, f32[512,128]{1,0:T(8,128)}, u32[]{:S(2)}) copy-start(f32[512,128]{1,0:T(8,128)} %copy-done.11) | copy-start | bytes 786436
  159.9 84.5 %all-gather.22.cloned.1.call-start = ((), (), s32[]{:S(2)}) async-start(), calls=%async_computation.8 | async-start | bytes 6303744 | tf_op jit(solution)/shard_map/all_gather | solution.py:38
  226.8 183.1 %all-gather.24.cloned.1.call-start = ((), (), s32[]{:S(2)}) async-start(), calls=%async_computation.9 | async-start | bytes 10506240 | tf_op jit(solution)/shard_map/all_gather | solution.py:38
  255.6 256.9 %all-gather.26.cloned.1.call-start = ((), (), s32[]{:S(2)}) async-start(), calls=%async_computation.10 | async-start | bytes 10506240 | tf_op jit(solution)/shard_map/all_gather | solution.py:38
  427.2 148.2 %all-gather.14.cloned.1.call-start = ((), (), s32[]{:S(2)}) async-start(), calls=%async_computation.4 | async-start | bytes 1179648 | tf_op jit(solution)/shard_map/all_gather | solution.py:195
  521.6 53.7 %copy-start.5 = (f32[1024,128]{1,0:T(8,128)S(1)}, f32[1024,128]{1,0:T(8,128)}, u32[]{:S(2)}) copy-start(f32[1024,128]{1,0:T(8,128)} %copy-done.4) | copy-start | bytes 1572868
  645.0 27.4 %all-to-all-start.2 = ((bf16[8,64,1024]{2,1,0:T(8,128)(2,1)}), bf16[8,64,1024]{2,1,0:T(8,128)(2,1)S(1)}, u32[]{:S(2)}, u32[]{:S(2)}) async-start(bf16[8,64,1024]{2,1,0:T(8,128)(2,1)} %stack.2), calls=%async_computation.2 | async-start | bytes 2097152 | tf_op jit(solution)/shard_map/all_to_all | solution.py:232
  672.9 16.8 %collective-permute-start = (bf16[512,128]{1,0:T(8,128)(2,1)S(1)}, bf16[512,128]{1,0:T(8,128)(2,1)S(1)}, u32[]{:S(2)}, u32[]{:S(2)}) collective-permute-start(bf16[512,128]{1,0:T(8,128)(2,1)S(1)} %convolution_convert_fusion.2), channel_id=1, source_target_pairs={{0,64},{8,72},{16,80},{24,88},{32,96},{40,104},{48,112},{56,120},{... | collective-permute-start | bytes 393224 | tf_op jit(solution)/shard_map/ppermute | solution.py:65
  676.0 17.4 %collective-permute-start.1 = (bf16[512,128]{1,0:T(8,128)(2,1)S(1)}, bf16[512,128]{1,0:T(8,128)(2,1)S(1)}, u32[]{:S(2)}, u32[]{:S(2)}) collective-permute-start(bf16[512,128]{1,0:T(8,128)(2,1)S(1)} %convolution_convert_fusion.2), channel_id=1, source_target_pairs={{0,56},{8,64},{16,72},{24,80},{32,88},{40,96},{48,104},{56,112},{6... | collective-permute-start | bytes 393224 | tf_op jit(solution)/shard_map/ppermute | solution.py:65
  679.8 15.9 %collective-permute-start.2 = (bf16[512,128]{1,0:T(8,128)(2,1)S(1)}, bf16[512,128]{1,0:T(8,128)(2,1)S(1)}, u32[]{:S(2)}, u32[]{:S(2)}) collective-permute-start(bf16[512,128]{1,0:T(8,128)(2,1)S(1)} %convolution_convert_fusion.2), channel_id=1, source_target_pairs={{0,48},{8,56},{16,64},{24,72},{32,80},{40,88},{48,96},{56,104},{64... | collective-permute-start | bytes 393224 | tf_op jit(solution)/shard_map/ppermute | solution.py:65
  681.1 18.3 %collective-permute-start.3 = (bf16[512,128]{1,0:T(8,128)(2,1)S(1)}, bf16[512,128]{1,0:T(8,128)(2,1)S(1)}, u32[]{:S(2)}, u32[]{:S(2)}) collective-permute-start(bf16[512,128]{1,0:T(8,128)(2,1)S(1)} %convolution_convert_fusion.2), channel_id=1, source_target_pairs={{0,40},{8,48},{16,56},{24,64},{32,72},{40,80},{48,88},{56,96},{64,... | collective-permute-start | bytes 393224 | tf_op jit(solution)/shard_map/ppermute | solution.py:65
  687.3 13.4 %collective-permute-start.4 = (bf16[512,128]{1,0:T(8,128)(2,1)S(1)}, bf16[512,128]{1,0:T(8,128)(2,1)S(1)}, u32[]{:S(2)}, u32[]{:S(2)}) collective-permute-start(bf16[512,128]{1,0:T(8,128)(2,1)S(1)} %convolution_convert_fusion.2), channel_id=1, source_target_pairs={{0,32},{8,40},{16,48},{24,56},{32,64},{40,72},{48,80},{56,88},{64,... | collective-permute-start | bytes 393224 | tf_op jit(solution)/shard_map/ppermute | solution.py:65
  689.7 12.9 %collective-permute-start.5 = (bf16[512,128]{1,0:T(8,128)(2,1)S(1)}, bf16[512,128]{1,0:T(8,128)(2,1)S(1)}, u32[]{:S(2)}, u32[]{:S(2)}) collective-permute-start(bf16[512,128]{1,0:T(8,128)(2,1)S(1)} %convolution_convert_fusion.2), channel_id=1, source_target_pairs={{0,24},{8,32},{16,40},{24,48},{32,56},{40,64},{48,72},{56,80},{64,... | collective-permute-start | bytes 393224 | tf_op jit(solution)/shard_map/ppermute | solution.py:65
  693.4 18.2 %collective-permute-start.6 = (bf16[512,128]{1,0:T(8,128)(2,1)S(1)}, bf16[512,128]{1,0:T(8,128)(2,1)S(1)}, u32[]{:S(2)}, u32[]{:S(2)}) collective-permute-start(bf16[512,128]{1,0:T(8,128)(2,1)S(1)} %convolution_convert_fusion.2), channel_id=1, source_target_pairs={{0,16},{8,24},{16,32},{24,40},{32,48},{40,56},{48,64},{56,72},{64,... | collective-permute-start | bytes 393224 | tf_op jit(solution)/shard_map/ppermute | solution.py:65
  695.7 17.2 %collective-permute-start.7 = (bf16[512,128]{1,0:T(8,128)(2,1)S(1)}, bf16[512,128]{1,0:T(8,128)(2,1)S(1)}, u32[]{:S(2)}, u32[]{:S(2)}) collective-permute-start(bf16[512,128]{1,0:T(8,128)(2,1)S(1)} %convolution_convert_fusion.2), channel_id=1, source_target_pairs={{0,8},{8,16},{16,24},{24,32},{32,40},{40,48},{48,56},{56,64},{64,7... | collective-permute-start | bytes 393224 | tf_op jit(solution)/shard_map/ppermute | solution.py:65
  699.4 25.8 %collective-permute-start.8 = (bf16[512,128]{1,0:T(8,128)(2,1)S(1)}, bf16[512,128]{1,0:T(8,128)(2,1)S(1)}, u32[]{:S(2)}, u32[]{:S(2)}) collective-permute-start(bf16[512,128]{1,0:T(8,128)(2,1)S(1)} %convolution_convert_fusion.1), channel_id=1, source_target_pairs={{0,64},{8,72},{16,80},{24,88},{32,96},{40,104},{48,112},{56,120},{... | collective-permute-start | bytes 393224 | tf_op jit(solution)/shard_map/ppermute | solution.py:65
  700.7 28.1 %collective-permute-start.9 = (bf16[512,128]{1,0:T(8,128)(2,1)S(1)}, bf16[512,128]{1,0:T(8,128)(2,1)S(1)}, u32[]{:S(2)}, u32[]{:S(2)}) collective-permute-start(bf16[512,128]{1,0:T(8,128)(2,1)S(1)} %convolution_convert_fusion.1), channel_id=1, source_target_pairs={{0,56},{8,64},{16,72},{24,80},{32,88},{40,96},{48,104},{56,112},{6... | collective-permute-start | bytes 393224 | tf_op jit(solution)/shard_map/ppermute | solution.py:65
  702.6 29.0 %collective-permute-start.10 = (bf16[512,128]{1,0:T(8,128)(2,1)S(1)}, bf16[512,128]{1,0:T(8,128)(2,1)S(1)}, u32[]{:S(2)}, u32[]{:S(2)}) collective-permute-start(bf16[512,128]{1,0:T(8,128)(2,1)S(1)} %convolution_convert_fusion.1), channel_id=1, source_target_pairs={{0,48},{8,56},{16,64},{24,72},{32,80},{40,88},{48,96},{56,104},{64... | collective-permute-start | bytes 393224 | tf_op jit(solution)/shard_map/ppermute | solution.py:65
  711.6 23.8 %collective-permute-start.11 = (bf16[512,128]{1,0:T(8,128)(2,1)S(1)}, bf16[512,128]{1,0:T(8,128)(2,1)S(1)}, u32[]{:S(2)}, u32[]{:S(2)}) collective-permute-start(bf16[512,128]{1,0:T(8,128)(2,1)S(1)} %convolution_convert_fusion.1), channel_id=1, source_target_pairs={{0,40},{8,48},{16,56},{24,64},{32,72},{40,80},{48,88},{56,96},{64,... | collective-permute-start | bytes 393224 | tf_op jit(solution)/shard_map/ppermute | solution.py:65
  712.9 22.5 %collective-permute-start.12 = (bf16[512,128]{1,0:T(8,128)(2,1)S(1)}, bf16[512,128]{1,0:T(8,128)(2,1)S(1)}, u32[]{:S(2)}, u32[]{:S(2)}) collective-permute-start(bf16[512,128]{1,0:T(8,128)(2,1)S(1)} %convolution_convert_fusion.1), channel_id=1, source_target_pairs={{0,32},{8,40},{16,48},{24,56},{32,64},{40,72},{48,80},{56,88},{64,... | collective-permute-start | bytes 393224 | tf_op jit(solution)/shard_map/ppermute | solution.py:65
  725.2 10.2 %collective-permute-start.13 = (bf16[512,128]{1,0:T(8,128)(2,1)S(1)}, bf16[512,128]{1,0:T(8,128)(2,1)S(1)}, u32[]{:S(2)}, u32[]{:S(2)}) collective-permute-start(bf16[512,128]{1,0:T(8,128)(2,1)S(1)} %convolution_convert_fusion.1), channel_id=1, source_target_pairs={{0,24},{8,32},{16,40},{24,48},{32,56},{40,64},{48,72},{56,80},{64,... | collective-permute-start | bytes 393224 | tf_op jit(solution)/shard_map/ppermute | solution.py:65
  728.8 6.9 collective-permute-start.14
  731.7 5.5 collective-permute-start.15
  (17 other events, 305.7 us)
Sparse Core Ops, SparseCore 0:
  9.9 61.7 all-gather.15
  83.1 75.1 all-gather.17
  160.9 57.3 all-gather.19
  226.9 17.4 all-gather.21
  255.7 154.1 all-gather.23
  427.3 85.1 all-gather.25
  515.0 60.2 all-gather.13
